TPU v7x, 32 devices: a whole 2x2x4 slice. The times are simulated.
32 devices in a mesh: wide: 8 (over z, x), narrow: 4 (over y, core).
Axes of the slice: x: 2, y: 2, z: 4, core: 2. Of those that a mesh axis runs over, the one named last changes fastest.
Arguments:
- activations: bfloat16 [2048, 16384], P('wide', 'narrow'), may hold values from -6 to 6
- grad_out: bfloat16 [2048, 8192], P('narrow', 'wide'), may hold values from -0.125 to 0.125
- momentum: float32 [8192, 16384], P('wide', 'narrow'), may hold values from -90 to 90
- right_factor: float32 [16384, 512], P('narrow'), may hold values from -0.046875 to 0.046875
Outputs:
- new_momentum: float32 [8192, 16384], P('wide', 'narrow')
- new_right: float32 [16384, 512], P('narrow')
- update: bfloat16 [8192, 16384], P('wide', 'narrow')
All inputs are finite; a program needn't handle non-finite values.
Results may differ from a plain program's by a relative error of at most 0.0012.
Values may be sent and summed in bfloat16 or wider, within the bound.
No kernel may reach another device: no remote copies, remote signals or barrier semaphores. Data moves between devices by JAX's collectives and lax.ppermute only.
A program may use at most 128 MiB of HBM per device.

v0:
```python
import math
import jax
import jax.numpy as jnp
from jax import lax
from jax.sharding import PartitionSpec as P

DOUT = 8192
DIN = 16384
RANK = 512
FEEDBACK = 0.05
EPSILON = 1e-06


def body(activations, grad_out, momentum, right_factor):
    highest = lax.Precision.HIGHEST
    out_rows = lax.all_gather(grad_out, "narrow", axis=0, tiled=True)
    gradient = lax.dot_general(
        out_rows,
        lax.all_gather(activations, "wide", axis=0, tiled=True),
        (((0,), (0,)), ((), ())),
        preferred_element_type=jnp.float32,
    )
    buffer = momentum + gradient
    partial_left = jnp.dot(
        buffer, right_factor, precision=highest, preferred_element_type=jnp.float32
    )
    left_factor = lax.psum(partial_left, "narrow")
    gram_local = jnp.dot(
        left_factor.T, left_factor, precision=highest, preferred_element_type=jnp.float32
    )
    gram_matrix = lax.psum(gram_local, "wide")
    lower_factor = jnp.linalg.cholesky(gram_matrix)
    ortho_left = jax.scipy.linalg.solve_triangular(lower_factor, left_factor.T, lower=True).T
    right_share = lax.psum_scatter(
        lax.dot_general(
            buffer,
            ortho_left,
            (((0,), (0,)), ((), ())),
            precision=highest,
            preferred_element_type=jnp.float32,
        ),
        "wide",
        scatter_dimension=0,
        tiled=True,
    )
    col_squares = lax.psum(jnp.sum(right_share * right_share, axis=0), ("wide", "narrow"))
    right_raw = lax.all_gather(right_share, "wide", axis=0, tiled=True)
    feedback = lax.dot_general(
        ortho_left,
        right_raw,
        (((1,), (1,)), ((), ())),
        precision=highest,
        preferred_element_type=jnp.float32,
    )
    new_momentum = buffer - FEEDBACK * feedback
    new_right = right_raw / (jnp.sqrt(col_squares) + EPSILON)
    update_scale = math.sqrt(DOUT * DIN / RANK)
    product = lax.dot_general(
        ortho_left,
        new_right,
        (((1,), (1,)), ((), ())),
        precision=highest,
        preferred_element_type=jnp.float32,
    )
    update = (update_scale * product).astype(jnp.bfloat16)
    return (new_momentum, new_right, update)


def solution(mesh):
    return jax.shard_map(
        body,
        mesh=mesh,
        in_specs=(P("wide", "narrow"), P("narrow", "wide"), P("wide", "narrow"), P("narrow", None)),
        out_specs=(P("wide", "narrow"), P("narrow", None), P("wide", "narrow")),
        check_vma=False,
    )
```

profile of v0, /device:TPU:0, one launch (start us, length us, event | category | flops | bytes accessed | tf_op | source)
XLA Modules:
  0.0 1089.3 jit_solution(18141778755275494876)
XLA Ops:
  7.2 0.7 all-gather.4.cloned.1.call-update
  7.9 0.7 all-gather.6.cloned.1.call-update
  8.7 38.1 %all-gather.4.cloned.1.call-done = bf16[2048,1024]{1,0:T(8,128)(2,1)} async-done(((bf16[512,1024]{1,0:T(8,128)(2,1)}), bf16[2048,1024]{1,0:T(8,128)(2,1)}) %all-gather.4.cloned.1.call-update) | async-done | bytes 4194320 | tf_op jit(solution)/shard_map/all_gather | solution.py:16
  46.7 229.4 %all-gather.6.cloned.1.call-done = bf16[2048,4096]{1,0:T(8,128)(2,1)} async-done(((bf16[256,4096]{1,0:T(8,128)(2,1)}), bf16[2048,4096]{1,0:T(8,128)(2,1)}) %all-gather.6.cloned.1.call-update) | async-done | bytes 16777232 | tf_op jit(solution)/shard_map/all_gather | solution.py:19
  276.2 28.3 %convolution_add_fusion = f32[1024,4096]{1,0:T(8,128)} fusion(f32[1024,4096]{1,0:T(8,128)} %param.6, bf16[2048,1024]{1,0:T(8,128)(2,1)} %all-gather.4.cloned.1.call-done, bf16[2048,4096]{1,0:T(8,128)(2,1)} %all-gather.6.cloned.1.call-done), kind=kOutput, calls=%fused_computation.4 | convolution fusion | flops 17184063488 | bytes 54525952 | tf_op jit(solution)/shard_map/dot_general | solution.py:17
  304.5 31.4 %fusion.39 = f32[1024,512]{1,0:T(8,128)} fusion(f32[1024,4096]{1,0:T(8,128)} %convolution_add_fusion, f32[4096,512]{1,0:T(8,128)} %param.7), kind=kOutput, calls=%fused_computation.78 | convolution fusion | flops 25769803776 | bytes 27262976 | tf_op jit(solution)/shard_map/dot_general | solution.py:24
  336.0 49.7 %all-reduce.4.cloned.1.call-done = f32[1024,512]{1,0:T(8,128)} async-done(((f32[1024,512]{1,0:T(8,128)}), f32[1024,512]{1,0:T(8,128)}) %all-reduce.4.cloned.1.call-update) | async-done | bytes 2097168 | tf_op jit(solution)/shard_map/psum | solution.py:27
  385.6 6.7 fusion.40
  392.6 78.3 %all-reduce.6.cloned.1.call-done = f32[512,512]{0,1:T(8,128)} async-done(((f32[512,512]{0,1:T(8,128)}), f32[512,512]{0,1:T(8,128)}) %all-reduce.6.cloned.1.call-update) | async-done | bytes 1048592 | tf_op jit(solution)/shard_map/psum | solution.py:31
  470.9 1.6 copy.8
  472.5 1.4 fusion.12
  473.9 1.0 copy-done.3
  474.9 11.7 %cholesky.104 = f32[128,128]{1,0:T(8,128)S(1)} custom-call(f32[128,128]{1,0:T(8,128)S(1)} %cholesky.266), custom_call_target="Cholesky" | custom-call | tf_op jit(solution)/shard_map/jit(cholesky)/cholesky | solution.py:32
  486.8 9.8 custom-call.31
  496.6 1.2 constant_dynamic-update-slice_fusion.3
  497.8 1.3 convolution_subtract_fusion.2
  499.1 11.7 %cholesky.217 = f32[128,128]{1,0:T(8,128)S(1)} custom-call(f32[128,128]{1,0:T(8,128)S(1)} %cholesky.270), custom_call_target="Cholesky" | custom-call | tf_op jit(solution)/shard_map/jit(cholesky)/cholesky | solution.py:32
  510.9 10.0 custom-call.32
  521.1 1.3 convolution_subtract_fusion.3
  522.5 11.7 %cholesky.238 = f32[128,128]{1,0:T(8,128)S(1)} custom-call(f32[128,128]{1,0:T(8,128)S(1)} %cholesky.275), custom_call_target="Cholesky" | custom-call | tf_op jit(solution)/shard_map/jit(cholesky)/cholesky | solution.py:32
  534.2 9.8 custom-call.33
  544.2 1.2 convolution_subtract_fusion.4
  545.5 11.7 %cholesky.255 = f32[128,128]{1,0:T(8,128)S(1)} custom-call(f32[128,128]{1,0:T(8,128)S(1)} %convolution_subtract_fusion.4), custom_call_target="Cholesky" | custom-call | tf_op jit(solution)/shard_map/jit(cholesky)/cholesky | solution.py:32
  557.2 0.7 compare_reduce_fusion.1
  558.5 0.7 compare_reduce_fusion.2
  561.7 1.6 select_select_fusion
  563.3 13.6 %while.1 = (s32[]{:T(128)}, f32[512,512]{1,0:T(8,128)}, s32[4,2]{0,1:T(2,128)S(1)}, f32[4,128,128]{2,1,0:T(8,128)}, s32[]{:T(128)}) while((s32[]{:T(128)}, f32[512,512]{1,0:T(8,128)}, s32[4,2]{0,1:T(2,128)S(1)}, f32[4,128,128]{2,1,0:T(8,128)}, s32[]{:T(128)}) %tuple.31), condition=%wide.while_cond, body=%wide.while_body.sunk | while | flops 2 | bytes 132205 | solution.py:33
  563.9 2.8 bitcast_dynamic-update-slice_fusion.2
  567.3 2.8 bitcast_dynamic-update-slice_fusion.2
  570.7 2.8 bitcast_dynamic-update-slice_fusion.2
  574.1 2.8 bitcast_dynamic-update-slice_fusion.2
  576.9 40.1 %custom-call.34 = f32[4,128,128]{1,2,0:T(8,128)S(1)} custom-call(f32[4,128,128]{2,1,0:T(8,128)} %get-tuple-element.10), custom_call_target="InvertDiagBlocksLowerTriangular" | custom-call | tf_op jit(solution)/shard_map/jit(_solve_triangular)/triangular_solve | solution.py:33
  617.0 0.6 fusion.13
  617.7 1.8 convolution_subtract_fusion.1
  619.5 0.6 fusion.27
  620.2 2.9 convolution_subtract_fusion
  623.0 0.6 fusion.25
  623.7 3.8 fusion.6
  627.5 0.6 fusion.24
  628.2 0.8 copy-done.4
  629.0 56.3 %fusion.15 = f32[4096,512]{1,0:T(8,128)} fusion(f32[1024,4096]{1,0:T(8,128)} %convolution_add_fusion, f32[128,1024]{1,0:T(8,128)S(1)} %fusion.24, f32[128,1024]{1,0:T(8,128)S(1)} %fusion.25, f32[128,1024]{1,0:T(8,128)S(1)} %fusion.27, f32[128,1024]{1,0:T(8,128)S(1)} %fusion.13), kind=kOutput, calls=%fused_computation.31 | convolution fusion | flops 25771376640 | bytes 27262976 | tf_op jit(solution)/shard_map/dot_general | solution.py:35
  685.4 147.2 %reduce-scatter.2.cloned.1.call-done = f32[512,512]{1,0:T(8,128)} async-done(((f32[4096,512]{1,0:T(8,128)}), f32[512,512]{1,0:T(8,128)}) %reduce-scatter.2.cloned.1.call-update) | async-done | bytes 1048592 | tf_op jit(solution)/shard_map/reduce_scatter | solution.py:34
  832.6 1.3 multiply_reduce_fusion
  833.9 43.3 %psum.23 = f32[512]{0:T(512)S(1)} all-reduce(f32[512]{0:T(512)S(1)} %multiply_reduce_fusion), channel_id=1, replica_groups=mesh['wide'=8,'narrow'=4] {'wide','narrow'}, use_global_device_ids=true, to_apply=%region_12.13 | all-reduce | flops 512 | bytes 4096 | tf_op jit(solution)/shard_map/psum | solution.py:46
  877.2 82.0 %all-gather.8.cloned.1.call-done = f32[4096,512]{1,0:T(8,128)} async-done(((f32[512,512]{1,0:T(8,128)}), f32[4096,512]{1,0:T(8,128)}) %all-gather.8.cloned.1.call-update) | async-done | bytes 8388624 | tf_op jit(solution)/shard_map/all_gather | solution.py:47
  959.2 8.9 broadcast_divide_fusion
  968.1 56.8 %multiply_convert_fusion = bf16[1024,4096]{1,0:T(8,128)(2,1)} fusion(f32[4096,512]{1,0:T(8,128)} %broadcast_divide_fusion, f32[128,1024]{1,0:T(8,128)} %copy-done.4, f32[128,1024]{1,0:T(8,128)} %copy-done.2, f32[128,1024]{1,0:T(8,128)} %copy-done.1, f32[128,1024]{1,0:T(8,128)S(1)} %fusion.13), kind=kOutput, calls=%fused_computation.2 | convolution fusion | flops 25779765248 | bytes 18874368 | tf_op jit(solution)/shard_map/dot_general | solution.py:58
  1025.0 57.3 %multiply_subtract_fusion = f32[1024,4096]{1,0:T(8,128)} fusion(f32[1024,4096]{1,0:T(8,128)S(1)} %bitcast.65, f32[4096,512]{1,0:T(8,128)S(1)} %bitcast.59, f32[128,1024]{1,0:T(8,128)} %copy-done.4, f32[128,1024]{1,0:T(8,128)} %copy-done.2, f32[128,1024]{1,0:T(8,128)} %copy-done.1, f32[128,1024]{1,0:T(8,128)S(1)} %fusion.13), kind=kOutput, calls=%fused_computation.3 | convolution fusion | flops 25779765248 | bytes 44040192 | tf_op jit(solution)/shard_map/dot_general | solution.py:48
  (55 shorter events, 4.3 us)
Async XLA Ops:
  7.2 39.6 %all-gather.4.cloned.1.call-start = ((), (), s32[]{:S(2)}) async-start(), calls=%async_computation.1 | async-start | bytes 5242880 | tf_op jit(solution)/shard_map/all_gather | solution.py:16
  7.9 268.3 %all-gather.6.cloned.1.call-start = ((), (), s32[]{:S(2)}) async-start(), calls=%async_computation.2 | async-start | bytes 18874368 | tf_op jit(solution)/shard_map/all_gather | solution.py:19
  8.6 377.0 %all-reduce.4.cloned.1.call-start = ((), (), s32[]{:S(2)}) async-start(), calls=%async_computation.3 | async-start | bytes 4194304 | tf_op jit(solution)/shard_map/psum | solution.py:27
  335.9 135.0 %all-reduce.6.cloned.1.call-start = ((), (), s32[]{:S(2)}) async-start(), calls=%async_computation.4 | async-start | bytes 2097152 | tf_op jit(solution)/shard_map/psum | solution.py:31
  392.4 440.2 %reduce-scatter.2.cloned.1.call-start = ((), (), s32[]{:S(2)}) async-start(), calls=%async_computation.5 | async-start | bytes 9437184 | tf_op jit(solution)/shard_map/reduce_scatter | solution.py:34
  473.9 1.0 copy-start.3
  474.9 142.1 %copy-start = (f32[1024,512]{1,0:T(8,128)S(1)}, f32[1024,512]{1,0:T(8,128)}, u32[]{:S(2)}) copy-start(f32[1024,512]{1,0:T(8,128)} %all-reduce.4.cloned.1.call-done) | copy-start | bytes 6291460
  620.2 65.1 %copy-start.1 = (f32[128,1024]{1,0:T(8,128)}, f32[128,1024]{1,0:T(8,128)S(1)}, u32[]{:S(2)}) copy-start(f32[128,1024]{1,0:T(8,128)S(1)} %fusion.27) | copy-start | bytes 1572868
  623.7 4.5 copy-start.2
  628.2 0.8 copy-start.4
  685.3 273.9 %all-gather.8.cloned.1.call-start = ((), (), s32[]{:S(2)}) async-start(), calls=%async_computation.6 | async-start | bytes 9437184 | tf_op jit(solution)/shard_map/all_gather | solution.py:47
  959.2 65.7 %slice-start = ((s8[8388608]{0:T(1024)(128)(4,1)}), s8[4194304]{0:T(1024)(128)(4,1)S(1)}, s32[]{:S(2)}) async-start(s8[8388608]{0:T(1024)(128)(4,1)} %bitcast.58), calls=%async_computation.7 | async-start | bytes 8388608
  959.2 65.7 %slice-start.2 = ((s8[16777216]{0:T(1024)(128)(4,1)}), s8[4194304]{0:T(1024)(128)(4,1)S(1)}, s32[]{:S(2)}) async-start(s8[16777216]{0:T(1024)(128)(4,1)} %bitcast.64), calls=%async_computation.9 | async-start | bytes 8388608
  959.2 65.7 %slice-start.3 = ((s8[16777216]{0:T(1024)(128)(4,1)}), s8[4194304]{0:T(1024)(128)(4,1)S(1)}, s32[]{:S(2)}) async-start(s8[16777216]{0:T(1024)(128)(4,1)} %bitcast.64), calls=%async_computation.10 | async-start | bytes 8388608
  968.1 56.8 %slice-start.1 = ((s8[8388608]{0:T(1024)(128)(4,1)}), s8[4194304]{0:T(1024)(128)(4,1)S(1)}, s32[]{:S(2)}) async-start(s8[8388608]{0:T(1024)(128)(4,1)} %bitcast.58), calls=%async_computation.8 | async-start | bytes 8388608
  968.1 56.8 %slice-start.4 = ((s8[16777216]{0:T(1024)(128)(4,1)}), s8[4194304]{0:T(1024)(128)(4,1)S(1)}, s32[]{:S(2)}) async-start(s8[16777216]{0:T(1024)(128)(4,1)} %bitcast.64), calls=%async_computation.11 | async-start | bytes 8388608
  968.1 56.8 %slice-start.5 = ((s8[16777216]{0:T(1024)(128)(4,1)}), s8[4194304]{0:T(1024)(128)(4,1)S(1)}, s32[]{:S(2)}) async-start(s8[16777216]{0:T(1024)(128)(4,1)} %bitcast.64), calls=%async_computation.12 | async-start | bytes 8388608
Sparse Core Ops, SparseCore 0:
  9.5 37.1 all-gather.3
  48.9 227.2 all-gather.5
  336.0 49.5 all-reduce.3
  392.5 78.3 all-reduce.5
  685.4 147.0 reduce-scatter.1
  834.5 124.6 all-gather.7
where the time goes:
time: 1100 us; the launch traced here: 1090 us
  waiting for transfers between devices  626 us (57%)
  matrix products  253 us (23%)
  other arithmetic  132 us (12%)
  blocking collectives  43.3 us (4%)
  local copies, waits for them, and re-layouts  17.1 us (2%)
  between operations  17.1 us (2%)
    all_gather x1, waiting for transfers between devices, body(): lax.all_gather(activations, 'wide', axis=0, tiled=True)  229 us
    reduce_scatter x1, waiting for transfers between devices, body(): lax.psum_scatter(lax.dot_general(buffer, ortho_left, (((0,), (0,)), ((),...  147 us
    all_gather x1, waiting for transfers between devices, body(): right_raw = lax.all_gather(right_share, 'wide', axis=0, tiled=True)  82 us
    another operation x14, other arithmetic, body(): lower_factor = jnp.linalg.cholesky(gram_matrix)  78.6 us
    psum x1, waiting for transfers between devices, body(): gram_matrix = lax.psum(gram_local, 'wide')  78.3 us
    dot_general x1, matrix products, body(): lax.dot_general(ortho_left, right_raw, (((1,), (1,)), ((), ())), precisio...  57.3 us
    dot_general x1, matrix products, body(): lax.dot_general(ortho_left, new_right, (((1,), (1,)), ((), ())), precisio...  56.8 us
    dot_general x1, matrix products, body(): lax.dot_general(buffer, ortho_left, (((0,), (0,)), ((), ())), precision=h...  56.3 us
  transfers between devices with their start and end apart: 6, of which 6 were waited for; matrix products, arithmetic and copies ran while one was open for 0% of the time, Pallas kernels for 0%

commit v1 on v0

--- a/solution.py
+++ b/solution.py
@@ -44,7 +44,8 @@
         tiled=True,
     )
     col_squares = lax.psum(jnp.sum(right_share * right_share, axis=0), ("wide", "narrow"))
-    right_raw = lax.all_gather(right_share, "wide", axis=0, tiled=True)
+    sent = jnp.stack([right_share] * lax.axis_size("wide"))
+    right_raw = jnp.concatenate(lax.all_to_all(sent, "wide", 0, 0), axis=0)
     feedback = lax.dot_general(
         ortho_left,
         right_raw,

time: 1100 us -> 1180 us (1.073)
  blocking collectives: 43.3 us -> 203 us
  waiting for transfers between devices: 626 us -> 544 us
    psum x1, blocking collectives: 43.3 us -> 203 us  [body(): lax.psum(jnp.sum(right_share * right_share, axis=0), ('wide', 'narrow'))]
    all_gather x1 -> x0, waiting for transfers between devices: 82 us -> none  [body(): right_raw = lax.all_gather(right_share, 'wide', axis=0, tiled=True)]
  transfers between devices with their start and end apart: 6 -> 6, of which waited for: 6 -> 5; matrix products, arithmetic and copies ran while one was open for 0% -> 0% of each run, Pallas kernels for 0% -> 0%
where the time goes in v1:
time: 1180 us; the launch traced here: 1170 us
  waiting for transfers between devices  544 us (46%)
  matrix products  252 us (21%)
  blocking collectives  203 us (17%)
  other arithmetic  126 us (11%)
  local copies, waits for them, and re-layouts  22.2 us (2%)
  between operations  16.7 us (1%)
    all_gather x1, waiting for transfers between devices, body(): lax.all_gather(activations, 'wide', axis=0, tiled=True)  229 us
    psum x1, blocking collectives, body(): lax.psum(jnp.sum(right_share * right_share, axis=0), ('wide', 'narrow'))  203 us
    reduce_scatter x1, waiting for transfers between devices, body(): lax.psum_scatter(lax.dot_general(buffer, ortho_left, (((0,), (0,)), ((),...  147 us
    another operation x14, other arithmetic, body(): lower_factor = jnp.linalg.cholesky(gram_matrix)  78.6 us
    psum x1, waiting for transfers between devices, body(): gram_matrix = lax.psum(gram_local, 'wide')  78.3 us
    dot_general x1, matrix products, body(): lax.dot_general(ortho_left, right_raw, (((1,), (1,)), ((), ())), precisio...  58.2 us
    dot_general x1, matrix products, body(): lax.dot_general(buffer, ortho_left, (((0,), (0,)), ((), ())), precision=h...  56.3 us
    dot_general x1, matrix products, body(): lax.dot_general(ortho_left, new_right, (((1,), (1,)), ((), ())), precisio...  54.3 us
  transfers between devices with their start and end apart: 6, of which 5 were waited for; matrix products, arithmetic and copies ran while one was open for 0% of the time, Pallas kernels for 0%

profile of v1, /device:TPU:0, one launch (start us, length us, event | category | flops | bytes accessed | tf_op | source)
XLA Modules:
  0.0 1169.5 jit_solution(12893448133682088445)
XLA Ops:
  7.2 0.7 all-gather.3.cloned.1.call-update
  7.9 0.7 all-gather.5.cloned.1.call-update
  8.7 38.1 %all-gather.3.cloned.1.call-done = bf16[2048,1024]{1,0:T(8,128)(2,1)} async-done(((bf16[512,1024]{1,0:T(8,128)(2,1)}), bf16[2048,1024]{1,0:T(8,128)(2,1)}) %all-gather.3.cloned.1.call-update) | async-done | bytes 4194320 | tf_op jit(solution)/shard_map/all_gather | solution.py:16
  46.7 229.4 %all-gather.5.cloned.1.call-done = bf16[2048,4096]{1,0:T(8,128)(2,1)} async-done(((bf16[256,4096]{1,0:T(8,128)(2,1)}), bf16[2048,4096]{1,0:T(8,128)(2,1)}) %all-gather.5.cloned.1.call-update) | async-done | bytes 16777232 | tf_op jit(solution)/shard_map/all_gather | solution.py:19
  276.2 28.3 %convolution_add_fusion = f32[1024,4096]{1,0:T(8,128)} fusion(f32[1024,4096]{1,0:T(8,128)} %param.6, bf16[2048,1024]{1,0:T(8,128)(2,1)} %all-gather.3.cloned.1.call-done, bf16[2048,4096]{1,0:T(8,128)(2,1)} %all-gather.5.cloned.1.call-done), kind=kOutput, calls=%fused_computation.4 | convolution fusion | flops 17184063488 | bytes 54525952 | tf_op jit(solution)/shard_map/dot_general | solution.py:17
  304.5 31.4 %fusion.39 = f32[1024,512]{1,0:T(8,128)} fusion(f32[1024,4096]{1,0:T(8,128)} %convolution_add_fusion, f32[4096,512]{1,0:T(8,128)} %param.7), kind=kOutput, calls=%fused_computation.78 | convolution fusion | flops 25769803776 | bytes 27262976 | tf_op jit(solution)/shard_map/dot_general | solution.py:24
  336.0 49.7 %all-reduce.4.cloned.1.call-done = f32[1024,512]{1,0:T(8,128)} async-done(((f32[1024,512]{1,0:T(8,128)}), f32[1024,512]{1,0:T(8,128)}) %all-reduce.4.cloned.1.call-update) | async-done | bytes 2097168 | tf_op jit(solution)/shard_map/psum | solution.py:27
  385.6 6.7 fusion.40
  392.6 78.3 %all-reduce.6.cloned.1.call-done = f32[512,512]{0,1:T(8,128)} async-done(((f32[512,512]{0,1:T(8,128)}), f32[512,512]{0,1:T(8,128)}) %all-reduce.6.cloned.1.call-update) | async-done | bytes 1048592 | tf_op jit(solution)/shard_map/psum | solution.py:31
  470.9 1.6 copy.8
  472.5 1.4 fusion.12
  473.9 1.0 copy-done.5
  474.9 11.7 %cholesky.104 = f32[128,128]{1,0:T(8,128)S(1)} custom-call(f32[128,128]{1,0:T(8,128)S(1)} %cholesky.266), custom_call_target="Cholesky" | custom-call | tf_op jit(solution)/shard_map/jit(cholesky)/cholesky | solution.py:32
  486.8 9.8 custom-call.31
  496.6 1.2 constant_dynamic-update-slice_fusion.3
  497.8 1.3 convolution_subtract_fusion.2
  499.1 11.7 %cholesky.217 = f32[128,128]{1,0:T(8,128)S(1)} custom-call(f32[128,128]{1,0:T(8,128)S(1)} %cholesky.270), custom_call_target="Cholesky" | custom-call | tf_op jit(solution)/shard_map/jit(cholesky)/cholesky | solution.py:32
  510.9 10.0 custom-call.32
  521.2 1.3 convolution_subtract_fusion.3
  522.5 11.7 %cholesky.238 = f32[128,128]{1,0:T(8,128)S(1)} custom-call(f32[128,128]{1,0:T(8,128)S(1)} %cholesky.275), custom_call_target="Cholesky" | custom-call | tf_op jit(solution)/shard_map/jit(cholesky)/cholesky | solution.py:32
  534.2 9.8 custom-call.33
  544.2 1.2 convolution_subtract_fusion.4
  545.5 11.7 %cholesky.255 = f32[128,128]{1,0:T(8,128)S(1)} custom-call(f32[128,128]{1,0:T(8,128)S(1)} %convolution_subtract_fusion.4), custom_call_target="Cholesky" | custom-call | tf_op jit(solution)/shard_map/jit(cholesky)/cholesky | solution.py:32
  557.2 0.6 compare_reduce_fusion.1
  557.9 0.7 compare_reduce_fusion
  558.5 0.6 compare_reduce_fusion.2
  561.7 1.6 select_select_fusion
  563.2 13.8 %while.1 = (s32[]{:T(128)}, f32[512,512]{1,0:T(8,128)}, s32[4,2]{0,1:T(2,128)S(1)}, f32[4,128,128]{2,1,0:T(8,128)}, s32[]{:T(128)}) while((s32[]{:T(128)}, f32[512,512]{1,0:T(8,128)}, s32[4,2]{0,1:T(2,128)S(1)}, f32[4,128,128]{2,1,0:T(8,128)}, s32[]{:T(128)}) %tuple.31), condition=%wide.while_cond, body=%wide.while_body.sunk | while | flops 2 | bytes 132205 | solution.py:33
  563.8 2.9 bitcast_dynamic-update-slice_fusion.2
  567.3 2.9 bitcast_dynamic-update-slice_fusion.2
  570.8 2.9 bitcast_dynamic-update-slice_fusion.2
  574.3 2.8 bitcast_dynamic-update-slice_fusion.2
  577.1 40.1 %custom-call.34 = f32[4,128,128]{1,2,0:T(8,128)S(1)} custom-call(f32[4,128,128]{2,1,0:T(8,128)} %get-tuple-element.10), custom_call_target="InvertDiagBlocksLowerTriangular" | custom-call | tf_op jit(solution)/shard_map/jit(_solve_triangular)/triangular_solve | solution.py:33
  617.2 0.6 fusion.13
  617.9 1.8 convolution_subtract_fusion.1
  619.7 0.6 fusion.27
  620.3 2.7 convolution_subtract_fusion
  623.1 0.6 fusion.25
  623.7 3.8 fusion.6
  627.6 0.6 fusion.24
  628.2 56.3 %fusion.15 = f32[4096,512]{1,0:T(8,128)} fusion(f32[1024,4096]{1,0:T(8,128)} %convolution_add_fusion, f32[128,1024]{1,0:T(8,128)S(1)} %fusion.24, f32[128,1024]{1,0:T(8,128)S(1)} %fusion.25, f32[128,1024]{1,0:T(8,128)S(1)} %fusion.27, f32[128,1024]{1,0:T(8,128)S(1)} %fusion.13), kind=kOutput, calls=%fused_computation.31 | convolution fusion | flops 25771376640 | bytes 27262976 | tf_op jit(solution)/shard_map/dot_general | solution.py:35
  684.5 147.2 %reduce-scatter.2.cloned.1.call-done = f32[512,512]{1,0:T(8,128)} async-done(((f32[4096,512]{1,0:T(8,128)}), f32[512,512]{1,0:T(8,128)}) %reduce-scatter.2.cloned.1.call-update) | async-done | bytes 1048592 | tf_op jit(solution)/shard_map/reduce_scatter | solution.py:34
  831.7 5.7 stack.2
  837.4 5.1 all-to-all-start
  842.7 203.1 %psum.23 = f32[512]{0:T(512)S(1)} all-reduce(f32[512]{0:T(512)S(1)} %multiply_reduce_fusion), channel_id=1, replica_groups=mesh['wide'=8,'narrow'=4] {'wide','narrow'}, use_global_device_ids=true, to_apply=%region_12.13 | all-reduce | flops 512 | bytes 4096 | tf_op jit(solution)/shard_map/psum | solution.py:46
  1045.8 58.2 %multiply_subtract_fusion = f32[1024,4096]{1,0:T(8,128)} fusion(f32[1024,4096]{1,0:T(8,128)} %convolution_add_fusion, f32[4096,512]{1,0:T(8,128)} %bitcast.12, f32[128,1024]{1,0:T(8,128)S(1)} %fusion.24, f32[128,1024]{1,0:T(8,128)S(1)} %copy-done.3, f32[128,1024]{1,0:T(8,128)S(1)} %fusion.27, f32[128,1024]{1,0:T(8,128)S(1)} %fusion.13), kind=kOutput, calls=%fused_computation.3 | convolution fusion | flops 25779765248 | bytes 44040192 | tf_op jit(solution)/shard_map/dot_general | solution.py:49
  1104.0 4.4 broadcast_divide_fusion
  1108.5 54.3 %multiply_convert_fusion = bf16[1024,4096]{1,0:T(8,128)(2,1)} fusion(f32[4096,512]{1,0:T(8,128)S(1)} %broadcast_divide_fusion, f32[128,1024]{1,0:T(8,128)S(1)} %fusion.24, f32[128,1024]{1,0:T(8,128)S(1)} %copy-done.3, f32[128,1024]{1,0:T(8,128)S(1)} %fusion.27, f32[128,1024]{1,0:T(8,128)S(1)} %fusion.13), kind=kOutput, calls=%fused_computation.2 | convolution fusion | flops 25779765248 | bytes 18874368 | tf_op jit(solution)/shard_map/dot_general | solution.py:59
  (43 shorter events, 3.8 us)
Async XLA Ops:
  7.2 39.6 %all-gather.3.cloned.1.call-start = ((), (), s32[]{:S(2)}) async-start(), calls=%async_computation.2 | async-start | bytes 5242880 | tf_op jit(solution)/shard_map/all_gather | solution.py:16
  7.9 268.3 %all-gather.5.cloned.1.call-start = ((), (), s32[]{:S(2)}) async-start(), calls=%async_computation.3 | async-start | bytes 18874368 | tf_op jit(solution)/shard_map/all_gather | solution.py:19
  8.6 377.0 %all-reduce.4.cloned.1.call-start = ((), (), s32[]{:S(2)}) async-start(), calls=%async_computation.4 | async-start | bytes 4194304 | tf_op jit(solution)/shard_map/psum | solution.py:27
  335.9 135.0 %all-reduce.6.cloned.1.call-start = ((), (), s32[]{:S(2)}) async-start(), calls=%async_computation.5 | async-start | bytes 2097152 | tf_op jit(solution)/shard_map/psum | solution.py:31
  392.4 439.4 %reduce-scatter.2.cloned.1.call-start = ((), (), s32[]{:S(2)}) async-start(), calls=%async_computation.6 | async-start | bytes 9437184 | tf_op jit(solution)/shard_map/reduce_scatter | solution.py:34
  473.9 1.0 copy-start.5
  474.9 142.3 %copy-start = (f32[1024,512]{1,0:T(8,128)S(1)}, f32[1024,512]{1,0:T(8,128)}, u32[]{:S(2)}) copy-start(f32[1024,512]{1,0:T(8,128)} %all-reduce.4.cloned.1.call-done) | copy-start | bytes 6291460
  623.7 4.5 copy-start.2
  837.4 5.1 copy-start.4
  837.4 208.3 %copy-start.3 = (f32[128,1024]{1,0:T(8,128)S(1)}, f32[128,1024]{1,0:T(8,128)}, u32[]{:S(2)}) copy-start(f32[128,1024]{1,0:T(8,128)} %copy-done.2) | copy-start | bytes 1572868
  837.4 208.3 %all-to-all-start = ((f32[8,512,512]{2,1,0:T(8,128)}), f32[8,512,512]{2,1,0:T(8,128)}, u32[]{:S(2)}, u32[]{:S(2)}) async-start(f32[8,512,512]{2,1,0:T(8,128)} %stack.2), calls=%async_computation.1 | async-start | bytes 16777216 | tf_op jit(solution)/shard_map/all_to_all | solution.py:48
  1108.5 54.3 %copy-start.1 = (f32[4096,512]{1,0:T(8,128)}, f32[4096,512]{1,0:T(8,128)S(1)}, u32[]{:S(2)}) copy-start(f32[4096,512]{1,0:T(8,128)S(1)} %broadcast_divide_fusion) | copy-start | bytes 25165828
Sparse Core Ops, SparseCore 0:
  9.5 37.1 all-gather.2
  48.9 227.2 all-gather.4
  336.0 49.5 all-reduce.3
  392.5 78.3 all-reduce.5
  684.7 147.0 reduce-scatter.1
